TPU v7x, 32 devices: a whole 2x2x4 slice. The times are simulated.
32 devices in a mesh: seq: 8 (over y, x, core), fsdp: 4 (over z).
Axes of the slice: x: 2, y: 2, z: 4, core: 2. Of those that a mesh axis runs over, the one named last changes fastest.
Arguments:
- hidden: bfloat16 [4096, 8192], P(('seq', 'fsdp')), may hold values from -6 to 6
- kv_blocks: bfloat16 [8192, 1024], P('fsdp'), may hold values from -0.0625 to 0.0625
- kv_scale: float32 [64, 8], P('fsdp'), may hold values from 0.5 to 2
- queries: bfloat16 [4096, 4096], P(('seq', 'fsdp')), may hold values from -24 to 24
- grad_out: bfloat16 [4096, 4096], P(('seq', 'fsdp')), may hold values from -6 to 6
Outputs:
- attn_out: bfloat16 [4096, 4096], P(('seq', 'fsdp'))
- grad_queries: bfloat16 [4096, 4096], P(('seq', 'fsdp'))
- grad_hidden: bfloat16 [4096, 8192], P(('seq', 'fsdp'))
- weight_grad: float32 [8192, 1024], P('fsdp')
All inputs are finite; a program needn't handle non-finite values.
Results may differ from a plain program's by a relative error of at most 0.0075.
The roundings to bfloat16 on the way count: a program that leaves them out, or rounds other values in their place, can miss the bound.
Values may be sent and summed in bfloat16 or wider, within the bound.
A program may use at most 128 MiB of HBM per device.

v0:
```python
import jax
import jax.numpy as jnp
from jax import lax
from jax.sharding import PartitionSpec as P

HEADS = 32
KV_HEADS = 4
HEAD = 128
QB = 128
NEG = -1e30


def shifted(block, axis, distance):
    devices = range(lax.axis_size(axis))
    route = [(i - distance, i) for i in devices if i - distance in devices]
    return lax.ppermute(block, axis, route)


def dequantize(blocks, scale):
    rows, cols = blocks.shape
    grid = blocks.astype(jnp.float32).reshape(scale.shape[0], QB, scale.shape[1], QB)
    return (grid * scale[:, None, :, None]).reshape(rows, cols).astype(jnp.bfloat16)


def attend_group(operands, allowed):
    qgrp, kgrp, vgrp, ggrp = operands
    factor = 1.0 / float(HEAD) ** 0.5
    scores = jnp.einsum("rhd,kd->rhk", qgrp, kgrp, preferred_element_type=jnp.float32) * factor
    scores = jnp.where(allowed[:, None, :], scores, NEG)
    top = jnp.max(scores, axis=-1, keepdims=True)
    expd = jnp.exp(scores - top)
    probs = expd / jnp.sum(expd, axis=-1, keepdims=True)
    probs_b = probs.astype(jnp.bfloat16)
    output = jnp.einsum("rhk,kd->rhd", probs_b, vgrp, preferred_element_type=jnp.float32).astype(
        jnp.bfloat16
    )
    dprobs = jnp.einsum("rhd,kd->rhk", ggrp, vgrp, preferred_element_type=jnp.float32)
    delta = jnp.sum(probs * dprobs, axis=-1, keepdims=True)
    dscores = (probs * (dprobs - delta) * factor).astype(jnp.bfloat16)
    gradq = jnp.einsum("rhk,kd->rhd", dscores, kgrp, preferred_element_type=jnp.float32).astype(
        jnp.bfloat16
    )
    gradk = jnp.einsum("rhk,rhd->kd", dscores, qgrp, preferred_element_type=jnp.float32)
    gradv = jnp.einsum("rhk,rhd->kd", probs_b, ggrp, preferred_element_type=jnp.float32)
    return (output, gradq, gradk, gradv)


def attend(queries, window, grad_out, allowed):
    rows = queries.shape[0]
    count = window.shape[0]
    group = HEADS // KV_HEADS
    kvw = KV_HEADS * HEAD
    qgrp = queries.reshape(rows, KV_HEADS, group, HEAD).transpose(1, 0, 2, 3)
    ggrp = grad_out.reshape(rows, KV_HEADS, group, HEAD).transpose(1, 0, 2, 3)
    kgrp = window[:, :kvw].reshape(count, KV_HEADS, HEAD).transpose(1, 0, 2)
    vgrp = window[:, kvw:].reshape(count, KV_HEADS, HEAD).transpose(1, 0, 2)
    output, gradq, gradk, gradv = lax.map(
        lambda ops: attend_group(ops, allowed), (qgrp, kgrp, vgrp, ggrp)
    )
    output = output.transpose(1, 0, 2, 3).reshape(rows, HEADS * HEAD)
    gradq = gradq.transpose(1, 0, 2, 3).reshape(rows, HEADS * HEAD)
    gradk = gradk.transpose(1, 0, 2).reshape(count, kvw)
    gradv = gradv.transpose(1, 0, 2).reshape(count, kvw)
    return (output, gradq, jnp.concatenate([gradk, gradv], axis=1))


def body(hidden, kv_blocks, kv_scale, queries, grad_out):
    tok = hidden.shape[0]
    groups = lax.axis_size("fsdp")
    reach = groups // 2
    place = lax.axis_index("fsdp")
    linear = lax.axis_index("seq") * groups + place
    weights = dequantize(kv_blocks, kv_scale)
    columns = lax.all_to_all(hidden, "fsdp", split_axis=1, concat_axis=0, tiled=True)
    rows = columns
    kv = lax.psum_scatter(
        jnp.dot(rows, weights, preferred_element_type=jnp.float32),
        "fsdp",
        scatter_dimension=0,
        tiled=True,
    ).astype(jnp.bfloat16)
    pieces = []
    for offset in range(reach, 0, -1):
        pieces.append(shifted(kv, ("seq", "fsdp"), offset))
    window = jnp.concatenate(pieces + [kv], axis=0)
    base = linear * tok
    qpos = base + jnp.arange(tok, dtype=jnp.int32)
    kpos = base - reach * tok + jnp.arange((reach + 1) * tok, dtype=jnp.int32)
    span = reach * tok
    allowed = (
        (qpos[:, None] - kpos[None, :] < span)
        & (kpos[None, :] <= qpos[:, None])
        & (kpos[None, :] >= 0)
    )
    attn_out, grad_queries, dwin = attend(queries, window, grad_out, allowed)
    total = dwin[reach * tok :]
    inside = total
    for offset in range(1, reach + 1):
        piece = dwin[(reach - offset) * tok : (reach - offset + 1) * tok]
        returned = shifted(piece, ("seq", "fsdp"), -offset)
        total = total + returned
        inside = inside + jnp.where(place + offset < groups, returned, jnp.zeros_like(returned))
    all_grad = total.astype(jnp.bfloat16)
    seg_grad = inside.astype(jnp.bfloat16)
    spread = lax.dot_general(
        lax.all_gather(seg_grad, "fsdp", axis=0, tiled=True),
        weights,
        (((1,), (1,)), ((), ())),
        preferred_element_type=jnp.float32,
    ).astype(jnp.bfloat16)
    grad_hidden = lax.all_to_all(spread, "fsdp", split_axis=0, concat_axis=1, tiled=True)
    rows = columns
    shard_grad = lax.dot_general(
        rows,
        lax.all_gather(all_grad, "fsdp", axis=0, tiled=True),
        (((0,), (0,)), ((), ())),
        preferred_element_type=jnp.float32,
    )
    weight_grad = lax.psum(shard_grad, "seq")
    return (attn_out, grad_queries, grad_hidden, weight_grad)


def solution(mesh):
    return jax.shard_map(
        body,
        mesh=mesh,
        in_specs=(
            P(("seq", "fsdp"), None),
            P("fsdp", None),
            P("fsdp", None),
            P(("seq", "fsdp"), None),
            P(("seq", "fsdp"), None),
        ),
        out_specs=(
            P(("seq", "fsdp"), None),
            P(("seq", "fsdp"), None),
            P(("seq", "fsdp"), None),
            P("fsdp", None),
        ),
        check_vma=False,
    )
```

profile of v0, /device:TPU:0, one launch (start us, length us, event | category | flops | bytes accessed | tf_op | source)
XLA Modules:
  0.0 503.2 jit_solution(12745964746301407682)
XLA Ops:
  7.2 4.1 copy.37
  11.2 6.5 %all-to-all-start = ((bf16[128,4,2048]{0,2,1:T(8,128)(2,1)}), bf16[128,4,2048]{0,2,1:T(8,128)(2,1)S(1)}, u32[]{:S(2)}, u32[]{:S(2)}) async-start(bf16[128,4,2048]{0,2,1:T(8,128)(2,1)} %bitcast.160), calls=%async_computation | async-start | bytes 4194304 | tf_op jit(solution)/shard_map/all_to_all | solution.py:74
  17.8 48.1 %all-to-all-done = bf16[128,4,2048]{0,2,1:T(8,128)(2,1)S(1)} async-done(((bf16[128,4,2048]{0,2,1:T(8,128)(2,1)}), bf16[128,4,2048]{0,2,1:T(8,128)(2,1)S(1)}, u32[]{:S(2)}, u32[]{:S(2)}) %all-to-all-start) | async-done | bytes 2097184 | tf_op jit(solution)/shard_map/all_to_all | solution.py:74
  65.9 2.6 copy.38
  68.5 0.6 mul.31
  69.1 4.2 copy-done
  73.4 1.0 copy-done.2
  74.4 4.0 convolution_bitcast_fusion.2
  78.5 42.8 %reduce-scatter.2.cloned.1.call-done = f32[128,1024]{0,1:T(8,128)} async-done(((f32[512,1024]{0,1:T(8,128)}), f32[128,1024]{0,1:T(8,128)}) %reduce-scatter.2.cloned.1.call-update) | async-done | bytes 524304 | tf_op jit(solution)/shard_map/reduce_scatter | solution.py:76
  121.3 1.1 convert_element_type.32
  122.4 2.6 collective-permute-start.1
  125.0 4.3 collective-permute-start
  129.3 1.3 copy.35
  130.6 1.6 copy.41
  132.3 3.2 collective-permute-done
  135.4 1.1 pad_maximum_fusion
  136.6 0.2 copy.39
  136.8 0.2 copy.40
  137.0 110.8 %while.17 = (s32[]{:T(128)}, bf16[4,128,8,128]{3,1,2,0:T(8,128)(2,1)}, bf16[4,128,8,128]{3,1,2,0:T(8,128)(2,1)}, f32[4,384,128]{1,2,0:T(8,128)S(1)}, f32[4,384,1...) while((s32[]{:T(128)}, ...), condition=%wide.region_5.6_spmd.clone, body=%wide.region_1.5_spmd.clone.sunk | while | flops 816830336 | bytes 25336436 | solution.py:57
  137.1 0.1 fusion.151
  137.2 3.0 fusion.152
  140.2 3.8 fusion.153
  143.9 1.3 fusion.154
  145.2 8.0 %fusion.155 = bf16[4,128,8,128]{3,1,2,0:T(8,128)(2,1)} fusion(bf16[4,128,8,128]{3,1,2,0:T(8,128)(2,1)} %get-tuple-element.254, s32[]{:T(128)S(6)} %copy.76, f32[128,8,384]{2,0,1:T(8,128)S(1)} %fusion.154, bf16[4,384,128]{2,1,0:T(8,128)(2,1)} %copy-done.9, f32[128,8,384]{2,0,1:T(8,128)} %get-tuple-element.238, f32[128,8]{0,1:T(8,128)S(1)} %get-tuple-element.237), kind=kOutput, calls=%fused_computation.16.clone.1 | convolution fusion | flops 103548288 | bytes 6661120 | tf_op jit(solution)/shard_map/while/body/eval_jaxpr/rhk,kd->rhd/dot_general | solution.py:40
  153.2 7.5 %fusion.156 = f32[4,384,128]{1,2,0:T(8,128)S(1)} fusion(f32[4,384,128]{1,2,0:T(8,128)S(1)} %get-tuple-element.255, s32[]{:T(128)S(6)} %copy.76, f32[128,8,384]{2,0,1:T(8,128)S(1)} %fusion.154, bf16[4,128,8,128]{1,3,2,0:T(8,128)(2,1)} %get-tuple-element.270, f32[128,8,384]{2,0,1:T(8,128)} %get-tuple-element.238, f32[128,8]{0,1:T(8,128)S(1)} %get-tuple-element.237), kind=kOutput, calls=%fused_computation.20.clone.1 | convolution fusion | flops 103417216 | bytes 6759424 | tf_op jit(solution)/shard_map/while/body/eval_jaxpr/rhk,rhd->kd/dot_general | solution.py:43
  160.7 4.0 fusion.157
  164.8 3.0 fusion.152
  167.8 3.8 fusion.153
  171.6 1.3 fusion.154
  172.9 8.0 %fusion.155 = bf16[4,128,8,128]{3,1,2,0:T(8,128)(2,1)} fusion(bf16[4,128,8,128]{3,1,2,0:T(8,128)(2,1)} %get-tuple-element.254, s32[]{:T(128)S(6)} %copy.76, f32[128,8,384]{2,0,1:T(8,128)S(1)} %fusion.154, bf16[4,384,128]{2,1,0:T(8,128)(2,1)} %copy-done.9, f32[128,8,384]{2,0,1:T(8,128)} %get-tuple-element.238, f32[128,8]{0,1:T(8,128)S(1)} %get-tuple-element.237), kind=kOutput, calls=%fused_computation.16.clone.1 | convolution fusion | flops 103548288 | bytes 6661120 | tf_op jit(solution)/shard_map/while/body/eval_jaxpr/rhk,kd->rhd/dot_general | solution.py:40
  180.9 7.5 %fusion.156 = f32[4,384,128]{1,2,0:T(8,128)S(1)} fusion(f32[4,384,128]{1,2,0:T(8,128)S(1)} %get-tuple-element.255, s32[]{:T(128)S(6)} %copy.76, f32[128,8,384]{2,0,1:T(8,128)S(1)} %fusion.154, bf16[4,128,8,128]{1,3,2,0:T(8,128)(2,1)} %get-tuple-element.270, f32[128,8,384]{2,0,1:T(8,128)} %get-tuple-element.238, f32[128,8]{0,1:T(8,128)S(1)} %get-tuple-element.237), kind=kOutput, calls=%fused_computation.20.clone.1 | convolution fusion | flops 103417216 | bytes 6759424 | tf_op jit(solution)/shard_map/while/body/eval_jaxpr/rhk,rhd->kd/dot_general | solution.py:43
  188.4 4.0 fusion.157
  192.5 3.0 fusion.152
  195.5 3.8 fusion.153
  199.3 1.3 fusion.154
  200.6 8.0 %fusion.155 = bf16[4,128,8,128]{3,1,2,0:T(8,128)(2,1)} fusion(bf16[4,128,8,128]{3,1,2,0:T(8,128)(2,1)} %get-tuple-element.254, s32[]{:T(128)S(6)} %copy.76, f32[128,8,384]{2,0,1:T(8,128)S(1)} %fusion.154, bf16[4,384,128]{2,1,0:T(8,128)(2,1)} %copy-done.9, f32[128,8,384]{2,0,1:T(8,128)} %get-tuple-element.238, f32[128,8]{0,1:T(8,128)S(1)} %get-tuple-element.237), kind=kOutput, calls=%fused_computation.16.clone.1 | convolution fusion | flops 103548288 | bytes 6661120 | tf_op jit(solution)/shard_map/while/body/eval_jaxpr/rhk,kd->rhd/dot_general | solution.py:40
  208.5 7.5 %fusion.156 = f32[4,384,128]{1,2,0:T(8,128)S(1)} fusion(f32[4,384,128]{1,2,0:T(8,128)S(1)} %get-tuple-element.255, s32[]{:T(128)S(6)} %copy.76, f32[128,8,384]{2,0,1:T(8,128)S(1)} %fusion.154, bf16[4,128,8,128]{1,3,2,0:T(8,128)(2,1)} %get-tuple-element.270, f32[128,8,384]{2,0,1:T(8,128)} %get-tuple-element.238, f32[128,8]{0,1:T(8,128)S(1)} %get-tuple-element.237), kind=kOutput, calls=%fused_computation.20.clone.1 | convolution fusion | flops 103417216 | bytes 6759424 | tf_op jit(solution)/shard_map/while/body/eval_jaxpr/rhk,rhd->kd/dot_general | solution.py:43
  216.1 4.0 fusion.157
  220.2 3.0 fusion.152
  223.2 3.8 fusion.153
  227.0 1.3 fusion.154
  228.3 8.0 %fusion.155 = bf16[4,128,8,128]{3,1,2,0:T(8,128)(2,1)} fusion(bf16[4,128,8,128]{3,1,2,0:T(8,128)(2,1)} %get-tuple-element.254, s32[]{:T(128)S(6)} %copy.76, f32[128,8,384]{2,0,1:T(8,128)S(1)} %fusion.154, bf16[4,384,128]{2,1,0:T(8,128)(2,1)} %copy-done.9, f32[128,8,384]{2,0,1:T(8,128)} %get-tuple-element.238, f32[128,8]{0,1:T(8,128)S(1)} %get-tuple-element.237), kind=kOutput, calls=%fused_computation.16.clone.1 | convolution fusion | flops 103548288 | bytes 6661120 | tf_op jit(solution)/shard_map/while/body/eval_jaxpr/rhk,kd->rhd/dot_general | solution.py:40
  236.2 7.5 %fusion.156 = f32[4,384,128]{1,2,0:T(8,128)S(1)} fusion(f32[4,384,128]{1,2,0:T(8,128)S(1)} %get-tuple-element.255, s32[]{:T(128)S(6)} %copy.76, f32[128,8,384]{2,0,1:T(8,128)S(1)} %fusion.154, bf16[4,128,8,128]{1,3,2,0:T(8,128)(2,1)} %get-tuple-element.270, f32[128,8,384]{2,0,1:T(8,128)} %get-tuple-element.238, f32[128,8]{0,1:T(8,128)S(1)} %get-tuple-element.237), kind=kOutput, calls=%fused_computation.20.clone.1 | convolution fusion | flops 103417216 | bytes 6759424 | tf_op jit(solution)/shard_map/while/body/eval_jaxpr/rhk,rhd->kd/dot_general | solution.py:43
  243.8 4.0 fusion.157
  247.8 1.9 fusion.98
  249.7 1.3 collective-permute-start.3
  251.0 1.3 collective-permute-start.2
  252.3 32.5 %collective-permute-done.3 = f32[128,1024]{0,1:T(8,128)} collective-permute-done((f32[128,1024]{0,1:T(8,128)}, f32[128,1024]{0,1:T(8,128)}, u32[]{:S(2)}, u32[]{:S(2)}) %collective-permute-start.3) | collective-permute-done | bytes 524320 | tf_op jit(solution)/shard_map/ppermute | solution.py:16
  284.8 2.4 add_convert_fusion
  287.3 0.7 all-gather.3.cloned.1.call-update
  288.0 0.3 all-reduce.2.cloned.1.call-start
  288.2 41.5 %all-gather.5.cloned.1.call-done = bf16[512,1024]{0,1:T(8,128)(2,1)} async-done(((bf16[128,1024]{0,1:T(8,128)(2,1)}), bf16[512,1024]{0,1:T(8,128)(2,1)}) %all-gather.5.cloned.1.call-update) | async-done | bytes 1048592 | tf_op jit(solution)/shard_map/all_gather | solution.py:115
  329.7 6.8 %convolution_bitcast_fusion.1 = f32[2048,1024]{0,1:T(8,128)} fusion(bf16[512,1024]{0,1:T(8,128)(2,1)} %all-gather.5.cloned.1.call-done, bf16[512,2048]{1,0:T(8,128)(2,1)S(1)} %bitcast.162), kind=kOutput, calls=%fused_computation.64 | convolution fusion | flops 2147483648 | bytes 11534336 | tf_op jit(solution)/shard_map/dot_general | solution.py:113
  336.5 23.0 %all-gather.3.cloned.1.call-done = bf16[512,1024]{0,1:T(8,128)(2,1)} async-done(((bf16[128,1024]{0,1:T(8,128)(2,1)}), bf16[512,1024]{0,1:T(8,128)(2,1)}) %all-gather.3.cloned.1.call-update) | async-done | bytes 1048592 | tf_op jit(solution)/shard_map/all_gather | solution.py:106
  359.6 9.0 %convolution_convert_fusion.1 = bf16[512,2048]{1,0:T(8,128)(2,1)} fusion(bf16[512,1024]{0,1:T(8,128)(2,1)} %all-gather.3.cloned.1.call-done, f32[256,8,8,128]{3,2,1,0:T(8,128)} %bitcast.157, bf16[2048,1024]{1,0:T(8,128)(2,1)} %param.8), kind=kOutput, calls=%fused_computation.65 | convolution fusion | flops 2154823680 | bytes 15728640 | tf_op jit(solution)/shard_map/dot_general | solution.py:105
  368.6 3.9 all-to-all-start.1
  372.5 0.7 copy.45
  373.2 0.6 copy-done.7
  373.8 0.7 copy.44
  374.5 2.2 copy_bitcast_fusion
  376.7 42.7 %all-to-all-done.1 = bf16[4,128,2048]{2,1,0:T(8,128)(2,1)S(1)} async-done(((bf16[4,128,2048]{2,1,0:T(8,128)(2,1)}), bf16[4,128,2048]{2,1,0:T(8,128)(2,1)S(1)}, u32[]{:S(2)}, u32[]{:S(2)}) %all-to-all-start.1) | async-done | bytes 2097184 | tf_op jit(solution)/shard_map/all_to_all | solution.py:111
  419.4 1.5 copy.58
  420.9 66.5 %all-reduce.2.cloned.1.call-done = f32[2048,1024]{0,1:T(8,128)} async-done(((f32[2048,1024]{0,1:T(8,128)}), f32[2048,1024]{0,1:T(8,128)}) %all-reduce.2.cloned.1.call-update) | async-done | bytes 8388624 | tf_op jit(solution)/shard_map/psum | solution.py:119
  487.4 9.2 %copy.49 = f32[2048,1024]{1,0:T(8,128)} copy(f32[2048,1024]{0,1:T(8,128)} %all-reduce.2.cloned.1.call-done) | data formatting | bytes 16777216
  (65 shorter events, 0.8 us)
Async XLA Ops:
  11.2 6.5 %copy-start.11 = (f32[16,8]{0,1:T(8,128)S(1)}, f32[16,8]{0,1:T(8,128)}, u32[]{:S(2)}) copy-start(f32[16,8]{0,1:T(8,128)} %param.9) | copy-start | bytes 1540
  11.2 54.7 %all-to-all-start = ((bf16[128,4,2048]{0,2,1:T(8,128)(2,1)}), bf16[128,4,2048]{0,2,1:T(8,128)(2,1)S(1)}, u32[]{:S(2)}, u32[]{:S(2)}) async-start(bf16[128,4,2048]{0,2,1:T(8,128)(2,1)} %bitcast.160), calls=%async_computation | async-start | bytes 4194304 | tf_op jit(solution)/shard_map/all_to_all | solution.py:74
  17.7 103.6 %reduce-scatter.2.cloned.1.call-start = ((), (), s32[]{:S(2)}) async-start(), calls=%async_computation.3 | async-start | bytes 2621440 | tf_op jit(solution)/shard_map/reduce_scatter | solution.py:76
  68.5 4.9 copy-start.1
  68.5 5.9 %copy-start.2 = (bf16[4,128,2048]{2,1,0:T(8,128)(2,1)S(1)}, bf16[4,128,2048]{2,1,0:T(8,128)(2,1)}, u32[]{:S(2)}) copy-start(bf16[4,128,2048]{2,1,0:T(8,128)(2,1)} %copy.38) | copy-start | bytes 6291460
  69.1 4.3 copy-start
  78.4 50.9 %copy-start.6 = (bf16[128,4096]{1,0:T(8,128)(2,1)S(1)}, bf16[128,4096]{1,0:T(8,128)(2,1)}, u32[]{:S(2)}) copy-start(bf16[128,4096]{1,0:T(8,128)(2,1)} %param.10) | copy-start | bytes 3145732
  78.4 251.3 %all-gather.5.cloned.1.call-start = ((), (), s32[]{:S(2)}) async-start(), calls=%async_computation.5 | async-start | bytes 1310720 | tf_op jit(solution)/shard_map/all_gather | solution.py:115
  122.4 9.8 %collective-permute-start.1 = (bf16[128,1024]{0,1:T(8,128)(2,1)S(1)}, bf16[128,1024]{0,1:T(8,128)(2,1)S(1)}, u32[]{:S(2)}, u32[]{:S(2)}) collective-permute-start(bf16[128,1024]{0,1:T(8,128)(2,1)S(1)} %convert_element_type.32), channel_id=1, source_target_pairs={{0,1},{1,2},{2,3},{3,4},{4,5},{5,6},{6,7},{7,8},{8,9},{9,10},{10,1... | collective-permute-start | bytes 786440 | tf_op jit(solution)/shard_map/ppermute | solution.py:16
  125.0 10.4 %collective-permute-start = (bf16[128,1024]{0,1:T(8,128)(2,1)S(1)}, bf16[128,1024]{0,1:T(8,128)(2,1)}, u32[]{:S(2)}, u32[]{:S(2)}) collective-permute-start(bf16[128,1024]{0,1:T(8,128)(2,1)S(1)} %convert_element_type.32), channel_id=1, source_target_pairs={{0,2},{1,3},{2,4},{3,5},{4,6},{5,7},{6,8},{7,9},{8,10},{9,11},{10,... | collective-permute-start | bytes 786440 | tf_op jit(solution)/shard_map/ppermute | solution.py:16
  137.0 6.9 %copy-start.4 = (bf16[4,384,128]{2,1,0:T(8,128)(2,1)}, bf16[4,384,128]{2,1,0:T(8,128)(2,1)S(1)}, u32[]{:S(2)}) copy-start(bf16[4,384,128]{2,1,0:T(8,128)(2,1)S(1)} %get-tuple-element.272) | copy-start | bytes 1179652 | tf_op jit(solution)/shard_map/while
  137.1 6.9 %copy-start.9 = (bf16[4,384,128]{2,1,0:T(8,128)(2,1)}, bf16[4,384,128]{2,1,0:T(8,128)(2,1)S(1)}, u32[]{:S(2)}) copy-start(bf16[4,384,128]{2,1,0:T(8,128)(2,1)S(1)} %get-tuple-element.271) | copy-start | bytes 1179652 | tf_op jit(solution)/shard_map/while
  160.7 4.0 copy-start.5
  160.7 4.0 copy-start.10
  164.7 6.9 %copy-start.4 = (bf16[4,384,128]{2,1,0:T(8,128)(2,1)}, bf16[4,384,128]{2,1,0:T(8,128)(2,1)S(1)}, u32[]{:S(2)}) copy-start(bf16[4,384,128]{2,1,0:T(8,128)(2,1)S(1)} %get-tuple-element.272) | copy-start | bytes 1179652 | tf_op jit(solution)/shard_map/while
  164.7 6.9 %copy-start.9 = (bf16[4,384,128]{2,1,0:T(8,128)(2,1)}, bf16[4,384,128]{2,1,0:T(8,128)(2,1)S(1)}, u32[]{:S(2)}) copy-start(bf16[4,384,128]{2,1,0:T(8,128)(2,1)S(1)} %get-tuple-element.271) | copy-start | bytes 1179652 | tf_op jit(solution)/shard_map/while
  188.4 4.0 copy-start.5
  188.4 4.0 copy-start.10
  192.4 6.9 %copy-start.4 = (bf16[4,384,128]{2,1,0:T(8,128)(2,1)}, bf16[4,384,128]{2,1,0:T(8,128)(2,1)S(1)}, u32[]{:S(2)}) copy-start(bf16[4,384,128]{2,1,0:T(8,128)(2,1)S(1)} %get-tuple-element.272) | copy-start | bytes 1179652 | tf_op jit(solution)/shard_map/while
  192.4 6.9 %copy-start.9 = (bf16[4,384,128]{2,1,0:T(8,128)(2,1)}, bf16[4,384,128]{2,1,0:T(8,128)(2,1)S(1)}, u32[]{:S(2)}) copy-start(bf16[4,384,128]{2,1,0:T(8,128)(2,1)S(1)} %get-tuple-element.271) | copy-start | bytes 1179652 | tf_op jit(solution)/shard_map/while
  216.1 4.0 copy-start.5
  216.1 4.0 copy-start.10
  220.1 6.9 %copy-start.4 = (bf16[4,384,128]{2,1,0:T(8,128)(2,1)}, bf16[4,384,128]{2,1,0:T(8,128)(2,1)S(1)}, u32[]{:S(2)}) copy-start(bf16[4,384,128]{2,1,0:T(8,128)(2,1)S(1)} %get-tuple-element.272) | copy-start | bytes 1179652 | tf_op jit(solution)/shard_map/while
  220.1 6.9 %copy-start.9 = (bf16[4,384,128]{2,1,0:T(8,128)(2,1)}, bf16[4,384,128]{2,1,0:T(8,128)(2,1)S(1)}, u32[]{:S(2)}) copy-start(bf16[4,384,128]{2,1,0:T(8,128)(2,1)S(1)} %get-tuple-element.271) | copy-start | bytes 1179652 | tf_op jit(solution)/shard_map/while
  243.8 4.0 copy-start.5
  243.8 4.0 copy-start.10
  249.7 35.1 %collective-permute-start.3 = (f32[128,1024]{0,1:T(8,128)}, f32[128,1024]{0,1:T(8,128)}, u32[]{:S(2)}, u32[]{:S(2)}) collective-permute-start(f32[128,1024]{0,1:T(8,128)} %get-tuple-element.157), channel_id=1, source_target_pairs={{2,0},{3,1},{4,2},{5,3},{6,4},{7,5},{8,6},{9,7},{10,8},{11,9},{12,... | collective-permute-start | bytes 1572872 | tf_op jit(solution)/shard_map/ppermute | solution.py:16
  251.0 33.8 %collective-permute-start.2 = (f32[128,1024]{0,1:T(8,128)S(1)}, f32[128,1024]{0,1:T(8,128)}, u32[]{:S(2)}, u32[]{:S(2)}) collective-permute-start(f32[128,1024]{0,1:T(8,128)S(1)} %get-tuple-element.156), channel_id=1, source_target_pairs={{1,0},{2,1},{3,2},{4,3},{5,4},{6,5},{7,6},{8,7},{9,8},{10,9},{11,1... | collective-permute-start | bytes 1572872 | tf_op jit(solution)/shard_map/ppermute | solution.py:16
  252.3 77.4 %copy-start.3 = (bf16[4,128,2048]{2,1,0:T(8,128)(2,1)S(1)}, bf16[4,128,2048]{2,1,0:T(8,128)(2,1)}, u32[]{:S(2)}) copy-start(bf16[4,128,2048]{2,1,0:T(8,128)(2,1)} %copy.38) | copy-start | bytes 6291460
  287.2 72.4 %all-gather.3.cloned.1.call-start = ((), (), s32[]{:S(2)}) async-start(), calls=%async_computation.4 | async-start | bytes 1310720 | tf_op jit(solution)/shard_map/all_gather | solution.py:106
  288.0 199.5 %all-reduce.2.cloned.1.call-start = ((), (), s32[]{:S(2)}) async-start(), calls=%async_computation.6 | async-start | bytes 16777216 | tf_op jit(solution)/shard_map/psum | solution.py:119
  368.6 3.9 copy-start.8
  368.6 50.8 %all-to-all-start.1 = ((bf16[4,128,2048]{2,1,0:T(8,128)(2,1)}), bf16[4,128,2048]{2,1,0:T(8,128)(2,1)S(1)}, u32[]{:S(2)}, u32[]{:S(2)}) async-start(bf16[4,128,2048]{2,1,0:T(8,128)(2,1)} %bitcast.18), calls=%async_computation.2 | async-start | bytes 4194304 | tf_op jit(solution)/shard_map/all_to_all | solution.py:111
  372.5 1.3 copy-start.7
Sparse Core Ops, SparseCore 0:
  78.6 42.7 reduce-scatter.1
  287.3 42.3 all-gather.4
  331.3 28.2 all-gather.2
  362.9 124.4 all-reduce.1
where the time goes:
time: 504 us; the launch traced here: 503 us
  waiting for transfers between devices  301 us (60%)
  matrix products  130 us (26%)
  local copies, waits for them, and re-layouts  31 us (6%)
  starting transfers between devices  20.2 us (4%)
  between operations  13.9 us (3%)
  other arithmetic  6.91 us (1%)
    psum x1, waiting for transfers between devices, body(): weight_grad = lax.psum(shard_grad, 'seq')  66.5 us
    all_to_all x1, waiting for transfers between devices, body(): lax.all_to_all(hidden, 'fsdp', split_axis=1, concat_axis=0, tiled=True)  48.1 us
    reduce_scatter x1, waiting for transfers between devices, body(): lax.psum_scatter(jnp.dot(rows, weights, preferred_element_type=jnp.float3...  42.8 us
    all_to_all x1, waiting for transfers between devices, body(): lax.all_to_all(spread, 'fsdp', split_axis=0, concat_axis=1, tiled=True)  42.7 us
    all_gather x1, waiting for transfers between devices, body(): lax.all_gather(all_grad, 'fsdp', axis=0, tiled=True)  41.5 us
    ppermute x4, waiting for transfers between devices, shifted(): return lax.ppermute(block, axis, route)  35.6 us
    dot_general x4, matrix products, attend_group(): jnp.einsum('rhk,kd->rhd', dscores, kgrp, preferred_element_type=jnp.float32)  31.9 us
    dot_general x4, matrix products, attend_group(): jnp.einsum('rhk,rhd->kd', dscores, qgrp, preferred_element_type=jnp.float32)  30 us
  transfers between devices with their start and end apart: 10, of which 8 were waited for; matrix products, arithmetic and copies ran while one was open for 5% of the time, Pallas kernels for 0%

commit v1 on v0

--- a/solution.py
+++ b/solution.py
@@ -8,6 +8,18 @@
 HEAD = 128
 QB = 128
 NEG = -1e30
+
+
+def in_blocks(shard, dim, peers):
+    lengths = shard.shape
+    blocks = shard.reshape(*lengths[:dim], peers, lengths[dim] // peers, *lengths[dim + 1 :])
+    return jnp.moveaxis(blocks, dim, 0)
+
+
+def laid_out(blocks, dim):
+    blocks = jnp.moveaxis(blocks, 0, dim)
+    lengths = blocks.shape
+    return blocks.reshape(*lengths[:dim], lengths[dim] * lengths[dim + 1], *lengths[dim + 2 :])
 
 
 def shifted(block, axis, distance):
@@ -71,7 +83,14 @@
     place = lax.axis_index("fsdp")
     linear = lax.axis_index("seq") * groups + place
     weights = dequantize(kv_blocks, kv_scale)
-    columns = lax.all_to_all(hidden, "fsdp", split_axis=1, concat_axis=0, tiled=True)
+    size, index = (lax.axis_size("fsdp"), lax.axis_index("fsdp"))
+    tiles = in_blocks(hidden, 1, size)
+    finished = [tiles[index]]
+    for step in range(1, size):
+        sent = tiles[index ^ step]
+        finished.append(lax.ppermute(sent, "fsdp", [(i_2, i_2 ^ step) for i_2 in range(size)]))
+    tiles = jnp.stack(finished)[index ^ jnp.arange(size)]
+    columns = laid_out(tiles, 0)
     rows = columns
     kv = lax.psum_scatter(
         jnp.dot(rows, weights, preferred_element_type=jnp.float32),

time: 504 us -> 505 us (level)
  local copies, waits for them, and re-layouts: 31 us -> 36.6 us
    all_to_all x1 -> x0, waiting for transfers between devices: 48.1 us -> none  [body(): lax.all_to_all(hidden, 'fsdp', split_axis=1, concat_axis=0, tiled=True)]
    ppermute x0 -> x3, waiting for transfers between devices: none -> 42.4 us  [body(): lax.ppermute(sent, 'fsdp', [(i_2, i_2 ^ step) for i_2 in range(size)])]
    all_to_all x1 -> x0, starting transfers between devices: 6.48 us -> none  [body(): lax.all_to_all(hidden, 'fsdp', split_axis=1, concat_axis=0, tiled=True)]
    ppermute x0 -> x3, starting transfers between devices: none -> 5.84 us  [body(): lax.ppermute(sent, 'fsdp', [(i_2, i_2 ^ step) for i_2 in range(size)])]
    unnamed x21 -> x32, local copies, waits for them, and re-layouts: 22.2 us -> 22.3 us
  transfers between devices with their start and end apart: 10 -> 12, of which waited for: 8 -> 9; matrix products, arithmetic and copies ran while one was open for 5% -> 5% of each run, Pallas kernels for 0% -> 0%
where the time goes in v1:
time: 505 us; the launch traced here: 503 us
  waiting for transfers between devices  297 us (59%)
  matrix products  127 us (25%)
  local copies, waits for them, and re-layouts  36.6 us (7%)
  starting transfers between devices  19.6 us (4%)
  between operations  14 us (3%)
  other arithmetic  8.94 us (2%)
    psum x1, waiting for transfers between devices, body(): weight_grad = lax.psum(shard_grad, 'seq')  66.5 us
    reduce_scatter x1, waiting for transfers between devices, body(): lax.psum_scatter(jnp.dot(rows, weights, preferred_element_type=jnp.float3...  43.8 us
    all_to_all x1, waiting for transfers between devices, body(): lax.all_to_all(spread, 'fsdp', split_axis=0, concat_axis=1, tiled=True)  42.7 us
    ppermute x3, waiting for transfers between devices, body(): lax.ppermute(sent, 'fsdp', [(i_2, i_2 ^ step) for i_2 in range(size)])  42.4 us
    all_gather x1, waiting for transfers between devices, body(): lax.all_gather(all_grad, 'fsdp', axis=0, tiled=True)  41.4 us
    ppermute x4, waiting for transfers between devices, shifted(): return lax.ppermute(block, axis, route)  36.7 us
    dot_general x4, matrix products, attend_group(): jnp.einsum('rhk,kd->rhd', dscores, kgrp, preferred_element_type=jnp.float32)  31.8 us
    dot_general x4, matrix products, attend_group(): jnp.einsum('rhk,rhd->kd', dscores, qgrp, preferred_element_type=jnp.float32)  30 us
  transfers between devices with their start and end apart: 12, of which 9 were waited for; matrix products, arithmetic and copies ran while one was open for 5% of the time, Pallas kernels for 0%

profile of v1, /device:TPU:0, one launch (start us, length us, event | category | flops | bytes accessed | tf_op | source)
XLA Modules:
  0.0 503.5 jit_solution(8354212331299904511)
XLA Ops:
  7.2 3.2 copy.34
  10.5 1.1 constant_dynamic-slice_fusion.3
  11.6 1.2 copy.38
  12.8 5.1 %collective-permute-start.2 = (bf16[128,2048]{1,0:T(8,128)(2,1)S(1)}, bf16[128,2048]{1,0:T(8,128)(2,1)S(1)}, u32[]{:S(2)}, u32[]{:S(2)}) collective-permute-start(bf16[128,2048]{1,0:T(8,128)(2,1)S(1)} %bitcast.190), channel_id=1, source_target_pairs={{0,3},{1,2},{2,1},{3,0},{4,7},{5,6},{6,5},{7,4},{8,11},{9,10},{10,... | collective-permute-start | bytes 1572872 | tf_op jit(solution)/shard_map/ppermute | solution.py:91
  18.0 1.3 copy.37
  20.5 10.4 %collective-permute-done.2 = bf16[128,2048]{1,0:T(8,128)(2,1)S(1)} collective-permute-done((bf16[128,2048]{1,0:T(8,128)(2,1)S(1)}, bf16[128,2048]{1,0:T(8,128)(2,1)S(1)}, u32[]{:S(2)}, u32[]{:S(2)}) %collective-permute-start.2) | collective-permute-done | bytes 524320 | tf_op jit(solution)/shard_map/ppermute | solution.py:91
  30.9 32.0 %collective-permute-done.1 = bf16[128,2048]{1,0:T(8,128)(2,1)} collective-permute-done((bf16[128,2048]{1,0:T(8,128)(2,1)S(1)}, bf16[128,2048]{1,0:T(8,128)(2,1)}, u32[]{:S(2)}, u32[]{:S(2)}) %collective-permute-start.1) | collective-permute-done | bytes 524320 | tf_op jit(solution)/shard_map/ppermute | solution.py:91
  62.9 1.6 pad_maximum_fusion
  64.5 2.0 gather_fusion
  67.1 4.2 copy-done
  71.4 1.0 copy-done.2
  72.4 4.0 fusion.102
  76.5 43.8 %reduce-scatter.2.cloned.1.call-done = f32[128,1024]{1,0:T(8,128)} async-done(((f32[512,1024]{1,0:T(8,128)}), f32[128,1024]{1,0:T(8,128)}) %reduce-scatter.2.cloned.1.call-update) | async-done | bytes 524304 | tf_op jit(solution)/shard_map/reduce_scatter | solution.py:95
  120.3 1.1 convert_element_type.32
  121.4 2.6 collective-permute-start.4
  124.0 4.3 collective-permute-start.3
  128.2 1.3 copy.33
  130.3 4.1 collective-permute-done.3
  134.4 1.0 pad_maximum_fusion.1
  136.8 111.6 %while.17 = (s32[]{:T(128)}, bf16[4,128,8,128]{3,1,2,0:T(8,128)(2,1)S(1)}, bf16[4,128,8,128]{3,1,2,0:T(8,128)(2,1)}, f32[4,384,128]{1,2,0:T(8,128)S(1)}, f32[4,3...) while((s32[]{:T(128)}, ...), condition=%wide.region_5.6_spmd.clone, body=%wide.region_1.5_spmd.clone.sunk | while | flops 816830336 | bytes 30579316 | solution.py:69
  136.9 2.9 fusion.154
  139.8 3.1 fusion.155
  142.9 1.0 copy-done.9
  143.9 1.3 fusion.156
  145.1 8.0 %fusion.157 = bf16[4,128,8,128]{3,1,2,0:T(8,128)(2,1)} fusion(bf16[4,128,8,128]{3,1,2,0:T(8,128)(2,1)} %get-tuple-element.246, s32[]{:T(128)S(6)} %copy.82, f32[128,8,384]{2,0,1:T(8,128)S(1)} %fusion.156, bf16[4,384,128]{2,1,0:T(8,128)(2,1)} %get-tuple-element.263, f32[128,8,384]{2,0,1:T(8,128)} %get-tuple-element.230, ...), kind=kOutput, calls=%fused_computation.17.clone.1 | convolution fusion | flops 103548288 | bytes 6661120 | tf_op jit(solution)/shard_map/while/body/eval_jaxpr/rhk,kd->rhd/dot_general | solution.py:52
  153.1 7.5 %fusion.158 = f32[4,384,128]{1,2,0:T(8,128)S(1)} fusion(f32[4,384,128]{1,2,0:T(8,128)S(1)} %get-tuple-element.247, s32[]{:T(128)S(6)} %copy.82, f32[128,8,384]{2,0,1:T(8,128)S(1)} %fusion.156, bf16[4,128,8,128]{1,3,2,0:T(8,128)(2,1)} %get-tuple-element.262, f32[128,8,384]{2,0,1:T(8,128)} %get-tuple-element.230, f32[128,8]{0,1:T(8,128)S(1)} %get-tuple-element.229), kind=kOutput, calls=%fused_computation.21.clone.1 | convolution fusion | flops 103417216 | bytes 6759424 | tf_op jit(solution)/shard_map/while/body/eval_jaxpr/rhk,rhd->kd/dot_general | solution.py:55
  160.7 4.0 fusion.159
  164.8 2.9 fusion.154
  167.7 3.1 fusion.155
  170.8 1.0 copy-done.9
  171.8 1.3 fusion.156
  173.1 7.9 %fusion.157 = bf16[4,128,8,128]{3,1,2,0:T(8,128)(2,1)} fusion(bf16[4,128,8,128]{3,1,2,0:T(8,128)(2,1)} %get-tuple-element.246, s32[]{:T(128)S(6)} %copy.82, f32[128,8,384]{2,0,1:T(8,128)S(1)} %fusion.156, bf16[4,384,128]{2,1,0:T(8,128)(2,1)} %get-tuple-element.263, f32[128,8,384]{2,0,1:T(8,128)} %get-tuple-element.230, ...), kind=kOutput, calls=%fused_computation.17.clone.1 | convolution fusion | flops 103548288 | bytes 6661120 | tf_op jit(solution)/shard_map/while/body/eval_jaxpr/rhk,kd->rhd/dot_general | solution.py:52
  181.0 7.5 %fusion.158 = f32[4,384,128]{1,2,0:T(8,128)S(1)} fusion(f32[4,384,128]{1,2,0:T(8,128)S(1)} %get-tuple-element.247, s32[]{:T(128)S(6)} %copy.82, f32[128,8,384]{2,0,1:T(8,128)S(1)} %fusion.156, bf16[4,128,8,128]{1,3,2,0:T(8,128)(2,1)} %get-tuple-element.262, f32[128,8,384]{2,0,1:T(8,128)} %get-tuple-element.230, f32[128,8]{0,1:T(8,128)S(1)} %get-tuple-element.229), kind=kOutput, calls=%fused_computation.21.clone.1 | convolution fusion | flops 103417216 | bytes 6759424 | tf_op jit(solution)/shard_map/while/body/eval_jaxpr/rhk,rhd->kd/dot_general | solution.py:55
  188.6 4.0 fusion.159
  192.7 2.9 fusion.154
  195.6 3.1 fusion.155
  198.7 1.0 copy-done.9
  199.7 1.3 fusion.156
  201.0 7.9 %fusion.157 = bf16[4,128,8,128]{3,1,2,0:T(8,128)(2,1)} fusion(bf16[4,128,8,128]{3,1,2,0:T(8,128)(2,1)} %get-tuple-element.246, s32[]{:T(128)S(6)} %copy.82, f32[128,8,384]{2,0,1:T(8,128)S(1)} %fusion.156, bf16[4,384,128]{2,1,0:T(8,128)(2,1)} %get-tuple-element.263, f32[128,8,384]{2,0,1:T(8,128)} %get-tuple-element.230, ...), kind=kOutput, calls=%fused_computation.17.clone.1 | convolution fusion | flops 103548288 | bytes 6661120 | tf_op jit(solution)/shard_map/while/body/eval_jaxpr/rhk,kd->rhd/dot_general | solution.py:52
  209.0 7.5 %fusion.158 = f32[4,384,128]{1,2,0:T(8,128)S(1)} fusion(f32[4,384,128]{1,2,0:T(8,128)S(1)} %get-tuple-element.247, s32[]{:T(128)S(6)} %copy.82, f32[128,8,384]{2,0,1:T(8,128)S(1)} %fusion.156, bf16[4,128,8,128]{1,3,2,0:T(8,128)(2,1)} %get-tuple-element.262, f32[128,8,384]{2,0,1:T(8,128)} %get-tuple-element.230, f32[128,8]{0,1:T(8,128)S(1)} %get-tuple-element.229), kind=kOutput, calls=%fused_computation.21.clone.1 | convolution fusion | flops 103417216 | bytes 6759424 | tf_op jit(solution)/shard_map/while/body/eval_jaxpr/rhk,rhd->kd/dot_general | solution.py:55
  216.5 4.0 fusion.159
  220.6 2.9 fusion.154
  223.5 3.1 fusion.155
  226.6 1.0 copy-done.9
  227.6 1.3 fusion.156
  228.9 7.9 %fusion.157 = bf16[4,128,8,128]{3,1,2,0:T(8,128)(2,1)} fusion(bf16[4,128,8,128]{3,1,2,0:T(8,128)(2,1)} %get-tuple-element.246, s32[]{:T(128)S(6)} %copy.82, f32[128,8,384]{2,0,1:T(8,128)S(1)} %fusion.156, bf16[4,384,128]{2,1,0:T(8,128)(2,1)} %get-tuple-element.263, f32[128,8,384]{2,0,1:T(8,128)} %get-tuple-element.230, ...), kind=kOutput, calls=%fused_computation.17.clone.1 | convolution fusion | flops 103548288 | bytes 6661120 | tf_op jit(solution)/shard_map/while/body/eval_jaxpr/rhk,kd->rhd/dot_general | solution.py:52
  236.8 7.5 %fusion.158 = f32[4,384,128]{1,2,0:T(8,128)S(1)} fusion(f32[4,384,128]{1,2,0:T(8,128)S(1)} %get-tuple-element.247, s32[]{:T(128)S(6)} %copy.82, f32[128,8,384]{2,0,1:T(8,128)S(1)} %fusion.156, bf16[4,128,8,128]{1,3,2,0:T(8,128)(2,1)} %get-tuple-element.262, f32[128,8,384]{2,0,1:T(8,128)} %get-tuple-element.230, f32[128,8]{0,1:T(8,128)S(1)} %get-tuple-element.229), kind=kOutput, calls=%fused_computation.21.clone.1 | convolution fusion | flops 103417216 | bytes 6759424 | tf_op jit(solution)/shard_map/while/body/eval_jaxpr/rhk,rhd->kd/dot_general | solution.py:55
  244.4 4.0 fusion.159
  248.4 2.5 fusion.98
  250.9 1.3 collective-permute-start.6
  252.2 1.3 collective-permute-start.5
  253.5 32.6 %collective-permute-done.6 = f32[128,1024]{0,1:T(8,128)} collective-permute-done((f32[128,1024]{0,1:T(8,128)}, f32[128,1024]{0,1:T(8,128)}, u32[]{:S(2)}, u32[]{:S(2)}) %collective-permute-start.6) | collective-permute-done | bytes 524320 | tf_op jit(solution)/shard_map/ppermute | solution.py:28
  286.1 2.3 add_convert_fusion
  289.4 41.4 %all-gather.5.cloned.1.call-done = bf16[512,1024]{0,1:T(8,128)(2,1)} async-done(((bf16[128,1024]{0,1:T(8,128)(2,1)}), bf16[512,1024]{0,1:T(8,128)(2,1)}) %all-gather.5.cloned.1.call-update) | async-done | bytes 1048592 | tf_op jit(solution)/shard_map/all_gather | solution.py:134
  330.8 6.9 %fusion.109 = f32[2048,1024]{1,0:T(8,128)} fusion(bf16[512,2048]{1,0:T(8,128)(2,1)S(1)} %bitcast.175, bf16[512,1024]{0,1:T(8,128)(2,1)} %all-gather.5.cloned.1.call-done), kind=kOutput, calls=%fused_computation.95 | convolution fusion | flops 2147483648 | bytes 11534336 | tf_op jit(solution)/shard_map/dot_general | solution.py:132
  337.7 22.9 %all-gather.3.cloned.1.call-done = bf16[512,1024]{0,1:T(8,128)(2,1)} async-done(((bf16[128,1024]{0,1:T(8,128)(2,1)}), bf16[512,1024]{0,1:T(8,128)(2,1)}) %all-gather.3.cloned.1.call-update) | async-done | bytes 1048592 | tf_op jit(solution)/shard_map/all_gather | solution.py:125
  360.6 9.0 %convolution_convert_fusion.1 = bf16[512,2048]{1,0:T(8,128)(2,1)} fusion(bf16[512,1024]{0,1:T(8,128)(2,1)} %all-gather.3.cloned.1.call-done, f32[256,8,8,128]{3,2,1,0:T(8,128)} %bitcast.171, bf16[2048,1024]{1,0:T(8,128)(2,1)} %param.8), kind=kOutput, calls=%fused_computation.65 | convolution fusion | flops 2154823680 | bytes 15728640 | tf_op jit(solution)/shard_map/dot_general | solution.py:124
  369.7 3.9 all-to-all-start
  374.3 1.4 copy.72
  376.4 1.4 copy.71
  377.8 42.7 %all-to-all-done = bf16[4,128,2048]{2,1,0:T(8,128)(2,1)S(1)} async-done(((bf16[4,128,2048]{2,1,0:T(8,128)(2,1)}), bf16[4,128,2048]{2,1,0:T(8,128)(2,1)S(1)}, u32[]{:S(2)}, u32[]{:S(2)}) %all-to-all-start) | async-done | bytes 2097184 | tf_op jit(solution)/shard_map/all_to_all | solution.py:130
  420.5 1.5 copy.60
  421.9 66.5 %all-reduce.2.cloned.1.call-done = f32[2048,1024]{1,0:T(8,128)} async-done(((f32[2048,1024]{1,0:T(8,128)}), f32[2048,1024]{1,0:T(8,128)}) %all-reduce.2.cloned.1.call-update) | async-done | bytes 8388624 | tf_op jit(solution)/shard_map/psum | solution.py:138
  488.5 8.4 %copy.95 = f32[2048,1024]{1,0:T(8,128)} copy(f32[2048,1024]{1,0:T(8,128)} %all-reduce.2.cloned.1.call-done) | data formatting | bytes 16777216
  (85 shorter events, 6.9 us)
Async XLA Ops:
  7.2 113.1 %reduce-scatter.2.cloned.1.call-start = ((), (), s32[]{:S(2)}) async-start(), calls=%async_computation.2 | async-start | bytes 2621440 | tf_op jit(solution)/shard_map/reduce_scatter | solution.py:95
  12.8 18.1 %collective-permute-start.2 = (bf16[128,2048]{1,0:T(8,128)(2,1)S(1)}, bf16[128,2048]{1,0:T(8,128)(2,1)S(1)}, u32[]{:S(2)}, u32[]{:S(2)}) collective-permute-start(bf16[128,2048]{1,0:T(8,128)(2,1)S(1)} %bitcast.190), channel_id=1, source_target_pairs={{0,3},{1,2},{2,1},{3,0},{4,7},{5,6},{6,5},{7,4},{8,11},{9,10},{10,... | collective-permute-start | bytes 1572872 | tf_op jit(solution)/shard_map/ppermute | solution.py:91
  18.0 2.4 copy-start.15
  19.2 43.6 %collective-permute-start.1 = (bf16[128,2048]{1,0:T(8,128)(2,1)S(1)}, bf16[128,2048]{1,0:T(8,128)(2,1)}, u32[]{:S(2)}, u32[]{:S(2)}) collective-permute-start(bf16[128,2048]{1,0:T(8,128)(2,1)S(1)} %bitcast.191), channel_id=1, source_target_pairs={{0,2},{1,3},{2,0},{3,1},{4,6},{5,7},{6,4},{7,5},{8,10},{9,11},{10,... | collective-permute-start | bytes 1572872 | tf_op jit(solution)/shard_map/ppermute | solution.py:91
  19.5 43.3 %collective-permute-start = (bf16[128,2048]{1,0:T(8,128)(2,1)S(1)}, bf16[128,2048]{1,0:T(8,128)(2,1)}, u32[]{:S(2)}, u32[]{:S(2)}) collective-permute-start(bf16[128,2048]{1,0:T(8,128)(2,1)S(1)} %bitcast.192), channel_id=1, source_target_pairs={{0,1},{1,0},{2,3},{3,2},{4,5},{5,4},{6,7},{7,6},{8,9},{9,8},{10,11... | collective-permute-start | bytes 1572872 | tf_op jit(solution)/shard_map/ppermute | solution.py:91
  30.9 32.0 %copy-start.14 = (bf16[128,2048]{1,0:T(8,128)(2,1)}, bf16[128,2048]{1,0:T(8,128)(2,1)S(1)}, u32[]{:S(2)}) copy-start(bf16[128,2048]{1,0:T(8,128)(2,1)S(1)} %collective-permute-done.2) | copy-start | bytes 1572868
  66.5 4.9 copy-start.1
  66.5 5.9 %copy-start.2 = (bf16[4,128,2048]{2,1,0:T(8,128)(2,1)S(1)}, bf16[4,128,2048]{2,1,0:T(8,128)(2,1)}, u32[]{:S(2)}) copy-start(bf16[4,128,2048]{2,1,0:T(8,128)(2,1)} %gather_fusion) | copy-start | bytes 6291460
  67.1 4.3 copy-start
  76.4 51.9 %copy-start.6 = (bf16[128,4096]{1,0:T(8,128)(2,1)S(1)}, bf16[128,4096]{1,0:T(8,128)(2,1)}, u32[]{:S(2)}) copy-start(bf16[128,4096]{1,0:T(8,128)(2,1)} %param.10) | copy-start | bytes 3145732
  76.4 53.2 %copy-start.7 = (bf16[128,4096]{1,0:T(8,128)(2,1)S(1)}, bf16[128,4096]{1,0:T(8,128)(2,1)}, u32[]{:S(2)}) copy-start(bf16[128,4096]{1,0:T(8,128)(2,1)} %param.11) | copy-start | bytes 3145732
  76.4 254.4 %all-gather.5.cloned.1.call-start = ((), (), s32[]{:S(2)}) async-start(), calls=%async_computation.4 | async-start | bytes 1310720 | tf_op jit(solution)/shard_map/all_gather | solution.py:134
  121.4 8.9 %collective-permute-start.4 = (bf16[128,1024]{1,0:T(8,128)(2,1)S(1)}, bf16[128,1024]{1,0:T(8,128)(2,1)S(1)}, u32[]{:S(2)}, u32[]{:S(2)}) collective-permute-start(bf16[128,1024]{1,0:T(8,128)(2,1)S(1)} %convert_element_type.32), channel_id=1, source_target_pairs={{0,1},{1,2},{2,3},{3,4},{4,5},{5,6},{6,7},{7,8},{8,9},{9,10},{10,1... | collective-permute-start | bytes 786440 | tf_op jit(solution)/shard_map/ppermute | solution.py:28
  124.0 10.4 %collective-permute-start.3 = (bf16[128,1024]{1,0:T(8,128)(2,1)S(1)}, bf16[128,1024]{1,0:T(8,128)(2,1)}, u32[]{:S(2)}, u32[]{:S(2)}) collective-permute-start(bf16[128,1024]{1,0:T(8,128)(2,1)S(1)} %convert_element_type.32), channel_id=1, source_target_pairs={{0,2},{1,3},{2,4},{3,5},{4,6},{5,7},{6,8},{7,9},{8,10},{9,11},{10,... | collective-permute-start | bytes 786440 | tf_op jit(solution)/shard_map/ppermute | solution.py:28
  135.4 1.4 copy-start.8
  136.8 6.1 %copy-start.4 = (bf16[4,384,128]{2,1,0:T(8,128)(2,1)}, bf16[4,384,128]{2,1,0:T(8,128)(2,1)S(1)}, u32[]{:S(2)}) copy-start(bf16[4,384,128]{2,1,0:T(8,128)(2,1)S(1)} %get-tuple-element.264) | copy-start | bytes 1179652 | tf_op jit(solution)/shard_map/while
  142.9 1.0 copy-start.9
  160.7 4.0 copy-start.5
  160.7 4.0 copy-start.10
  164.7 6.1 %copy-start.4 = (bf16[4,384,128]{2,1,0:T(8,128)(2,1)}, bf16[4,384,128]{2,1,0:T(8,128)(2,1)S(1)}, u32[]{:S(2)}) copy-start(bf16[4,384,128]{2,1,0:T(8,128)(2,1)S(1)} %get-tuple-element.264) | copy-start | bytes 1179652 | tf_op jit(solution)/shard_map/while
  170.8 1.0 copy-start.9
  188.5 4.1 copy-start.5
  188.5 4.1 copy-start.10
  192.6 6.1 %copy-start.4 = (bf16[4,384,128]{2,1,0:T(8,128)(2,1)}, bf16[4,384,128]{2,1,0:T(8,128)(2,1)S(1)}, u32[]{:S(2)}) copy-start(bf16[4,384,128]{2,1,0:T(8,128)(2,1)S(1)} %get-tuple-element.264) | copy-start | bytes 1179652 | tf_op jit(solution)/shard_map/while
  198.7 1.0 copy-start.9
  216.5 4.0 copy-start.5
  216.5 4.0 copy-start.10
  220.5 6.1 %copy-start.4 = (bf16[4,384,128]{2,1,0:T(8,128)(2,1)}, bf16[4,384,128]{2,1,0:T(8,128)(2,1)S(1)}, u32[]{:S(2)}) copy-start(bf16[4,384,128]{2,1,0:T(8,128)(2,1)S(1)} %get-tuple-element.264) | copy-start | bytes 1179652 | tf_op jit(solution)/shard_map/while
  226.6 1.0 copy-start.9
  244.4 4.0 copy-start.5
  244.4 4.0 copy-start.10
  248.4 5.1 %copy-start.11 = (bf16[4,128,8,128]{3,1,2,0:T(8,128)(2,1)}, bf16[4,128,8,128]{3,1,2,0:T(8,128)(2,1)S(1)}, u32[]{:S(2)}) copy-start(bf16[4,128,8,128]{3,1,2,0:T(8,128)(2,1)S(1)} %get-tuple-element.59) | copy-start | bytes 3145732
  250.9 35.2 %collective-permute-start.6 = (f32[128,1024]{0,1:T(8,128)}, f32[128,1024]{0,1:T(8,128)}, u32[]{:S(2)}, u32[]{:S(2)}) collective-permute-start(f32[128,1024]{0,1:T(8,128)} %get-tuple-element.149), channel_id=1, source_target_pairs={{2,0},{3,1},{4,2},{5,3},{6,4},{7,5},{8,6},{9,7},{10,8},{11,9},{12,... | collective-permute-start | bytes 1572872 | tf_op jit(solution)/shard_map/ppermute | solution.py:28
  252.2 33.9 %collective-permute-start.5 = (f32[128,1024]{0,1:T(8,128)}, f32[128,1024]{0,1:T(8,128)}, u32[]{:S(2)}, u32[]{:S(2)}) collective-permute-start(f32[128,1024]{0,1:T(8,128)} %get-tuple-element.148), channel_id=1, source_target_pairs={{1,0},{2,1},{3,2},{4,3},{5,4},{6,5},{7,6},{8,7},{9,8},{10,9},{11,1... | collective-permute-start | bytes 1572872 | tf_op jit(solution)/shard_map/ppermute | solution.py:28
  253.5 77.3 %copy-start.3 = (bf16[4,128,2048]{2,1,0:T(8,128)(2,1)S(1)}, bf16[4,128,2048]{2,1,0:T(8,128)(2,1)}, u32[]{:S(2)}) copy-start(bf16[4,128,2048]{2,1,0:T(8,128)(2,1)} %gather_fusion) | copy-start | bytes 6291460
  288.4 72.3 %all-gather.3.cloned.1.call-start = ((), (), s32[]{:S(2)}) async-start(), calls=%async_computation.3 | async-start | bytes 1310720 | tf_op jit(solution)/shard_map/all_gather | solution.py:125
  289.1 199.4 %all-reduce.2.cloned.1.call-start = ((), (), s32[]{:S(2)}) async-start(), calls=%async_computation.5 | async-start | bytes 16777216 | tf_op jit(solution)/shard_map/psum | solution.py:138
  369.7 3.9 copy-start.12
  369.7 50.8 %all-to-all-start = ((bf16[4,128,2048]{2,1,0:T(8,128)(2,1)}), bf16[4,128,2048]{2,1,0:T(8,128)(2,1)S(1)}, u32[]{:S(2)}, u32[]{:S(2)}) async-start(bf16[4,128,2048]{2,1,0:T(8,128)(2,1)} %bitcast.22), calls=%async_computation.1 | async-start | bytes 4194304 | tf_op jit(solution)/shard_map/all_to_all | solution.py:130
  374.3 1.4 copy-start.13
Sparse Core Ops, SparseCore 0:
  76.5 43.7 reduce-scatter.1
  288.5 42.2 all-gather.4
  332.4 28.2 all-gather.2
  364.0 124.4 all-reduce.1
